TPU v7x, 32 devices: a whole 2x2x4 slice. The times are simulated.
32 devices in a mesh: gx: 8 (over z, x), gy: 4 (over y, core).
Axes of the slice: x: 2, y: 2, z: 4, core: 2. Of those that a mesh axis runs over, the one named last changes fastest.
Arguments:
- parcel_props: float32 [16, 131072], P(None, ('gx', 'gy')), may hold values from -6 to 6
- size_class: int32 [131072], P(('gx', 'gy')), may hold values from 0 to 7
- dest_owner: int32 [131072, 1], P(('gx', 'gy')), may hold values from 0 to 31; in each aligned block of 4096 rows (0 to 4095, 4096 to 8191, ...) at most 512 rows name the same one
- dest_local: int32 [131072], P(('gx', 'gy')), may hold values from 0 to 4095
- class_table: float32 [8, 16], replicated, may hold values from 0.5 to 2
- gas_density: float32 [256, 512], P('gx', 'gy'), may hold values from 0.5 to 2
- gas_rest: float32 [4, 256, 512], P(None, 'gx', 'gy'), may hold values from -6 to 6
Outputs:
- new_density: float32 [256, 512], P('gx', 'gy')
- new_rest: float32 [4, 256, 512], P(None, 'gx', 'gy')
Inputs may be any that keep to these rules, and one draw needn't show every extreme that they name: `dest_owner`: among the parcels of one device, no owner device is named by more than 512 of them, a bound that some block reaches.
All inputs are finite; a program needn't handle non-finite values.
Results may differ from a plain program's by a relative error of at most 0.00015.
Values sent between devices are 32-bit elements; how exact they have to be, the bound alone decides.
No kernel may reach another device: no remote copies, remote signals or barrier semaphores. Data moves between devices by JAX's collectives and lax.ppermute only.
A program may use at most 64 MiB of HBM per device.

v0:
```python
import math
import jax
import jax.numpy as jnp
from jax import lax
from jax.sharding import PartitionSpec as P


def with_halo(shard, sides, width):
    for axis, dim in sides:
        devices, length = (lax.axis_size(axis), shard.shape[dim])
        up = [(i, (i + 1) % devices) for i in range(devices - 1)]
        down = [(j, i) for i, j in up]
        last = lax.slice_in_dim(shard, length - width, length, axis=dim)
        leading = lax.slice_in_dim(shard, 0, width, axis=dim)
        before = lax.ppermute(last, axis, up)
        after = lax.ppermute(leading, axis, down)
        shard = jnp.concatenate([before, shard, after], axis=dim)
    return shard


def sources_of(props, classes, gas, table):
    count = table.shape[0]
    picks = (classes[None, :] == jnp.arange(count, dtype=jnp.int32)[:, None]).astype(jnp.float32)
    coef = jnp.dot(
        table.T, picks, precision=lax.Precision.HIGHEST, preferred_element_type=jnp.float32
    )
    mass = jnp.exp(0.5 * props[0])
    density = gas[0]
    velocity = gas[1:4] / density
    theta = gas[4] / density
    slip = props[1:4] - velocity
    rate = coef[0] * jax.nn.softplus(props[4] - theta)
    evapor = mass * (1.0 - jnp.exp(-rate))
    dragged = 1.0 - jnp.exp(-coef[1] * jnp.sqrt(1.0 + jnp.sum(slip * slip, axis=0)))
    moment = evapor * coef[2:5] * props[1:4] + mass * dragged * slip
    energy = evapor * (props[4] + jnp.sum(coef[5:] * props[5:], axis=0))
    return jnp.concatenate([evapor[None], moment, energy[None]], axis=0)


def cell_hot(cells, first, width):
    return (cells[None, :] == (first + jnp.arange(width, dtype=jnp.int32))[:, None]).astype(
        jnp.float32
    )


def look_up(table, cells):
    total = table.shape[1]
    width = math.gcd(total, 512)

    def look_advance(index, gathered):
        first = (index * width).astype(jnp.int32)
        block = lax.dynamic_slice_in_dim(table, first, width, 1)
        return gathered + jnp.dot(
            block,
            cell_hot(cells, first, width),
            precision=lax.Precision.HIGHEST,
            preferred_element_type=jnp.float32,
        )

    return lax.fori_loop(
        0, total // width, look_advance, jnp.zeros((table.shape[0], cells.shape[0]), jnp.float32)
    )


def deposit_into(source, cells, total):
    width = math.gcd(total, 512)

    def deposit_advance(index, field):
        first = (index * width).astype(jnp.int32)
        block = lax.dot_general(
            source,
            cell_hot(cells, first, width),
            (((1,), (1,)), ((), ())),
            precision=lax.Precision.HIGHEST,
            preferred_element_type=jnp.float32,
        )
        return lax.dynamic_update_slice_in_dim(field, block, first, 1)

    return lax.fori_loop(
        0, total // width, deposit_advance, jnp.zeros((source.shape[0], total), jnp.float32)
    )


def per_device(
    parcel_props, size_class, dest_owner, dest_local, class_table, gas_density, gas_rest
):
    width_x = lax.axis_size("gx")
    width_y = lax.axis_size("gy")
    devices = width_x * width_y
    parcels = parcel_props.shape[1]
    slab_x, slab_y = gas_density.shape
    capacity = max(2, 4 * parcels // devices)
    slots = devices * capacity
    owner = dest_owner[:, 0]
    member = (owner[:, None] == jnp.arange(devices, dtype=jnp.int32)[None, :]).astype(jnp.int32)
    rank = jnp.sum(jnp.cumsum(member, axis=0) * member, axis=1) - 1
    slot = owner * capacity + rank
    gas_flat = jnp.concatenate([gas_density[None], gas_rest], axis=0).reshape(5, slab_x * slab_y)
    float_buf = jnp.zeros((parcel_props.shape[0], slots), jnp.float32).at[:, slot].set(parcel_props)
    int_buf = (
        jnp.full((2, slots), -1, jnp.int32).at[:, slot].set(jnp.stack([size_class, dest_local]))
    )
    got_floats, got_ints = (
        lax.all_to_all(
            lax.all_to_all(
                float_buf.reshape(-1, width_x, width_y, capacity),
                "gx",
                split_axis=1,
                concat_axis=1,
                tiled=True,
            ),
            "gy",
            split_axis=2,
            concat_axis=2,
            tiled=True,
        ),
        lax.all_to_all(
            lax.all_to_all(
                int_buf.reshape(2, width_x, width_y, capacity),
                "gx",
                split_axis=1,
                concat_axis=1,
                tiled=True,
            ),
            "gy",
            split_axis=2,
            concat_axis=2,
            tiled=True,
        ),
    )
    props_in = got_floats.reshape(parcel_props.shape[0], slots)
    ints_in = got_ints.reshape(2, slots)
    cells = ints_in[1]
    safe = jnp.maximum(cells, 0)
    source = sources_of(props_in, ints_in[0], look_up(gas_flat, safe), class_table)
    deposit = deposit_into(source, cells, slab_x * slab_y).reshape(5, slab_x, slab_y)
    padded = with_halo(deposit, (("gx", 1), ("gy", 2)), 1)
    beside = padded[:, 2:, 1:-1] + padded[:, :-2, 1:-1] + padded[:, 1:-1, 2:] + padded[:, 1:-1, :-2]
    smooth = 0.4 * deposit + 0.15 * beside
    return (gas_density + smooth[0], gas_rest + smooth[1:])


def solution(mesh):
    return jax.shard_map(
        per_device,
        mesh=mesh,
        in_specs=(
            P(None, ("gx", "gy")),
            P(("gx", "gy")),
            P(("gx", "gy"), None),
            P(("gx", "gy")),
            P(),
            P("gx", "gy"),
            P(None, "gx", "gy"),
        ),
        out_specs=(P("gx", "gy"), P(None, "gx", "gy")),
        check_vma=False,
    )
```

profile of v0, /device:TPU:9, one launch (start us, length us, event | category | flops | bytes accessed | tf_op | source)
XLA Modules:
  0.0 324.7 jit_solution(1331157601480989141)
XLA Ops:
  0.6 0.8 fusion.26
  1.4 9.2 %reduce-window.6 = s32[32,32,128]{2,1,0:T(8,128)S(1)} reduce-window(s32[32,32,128]{2,1,0:T(8,128)S(1)} %fusion.26, s32[]{:T(128)} %constant.78.clone.1), window={size=1x1x128 pad=0_0x0_0x127_0}, to_apply=%region_0.0 | reduce-window | flops 16646144 | bytes 1048580 | tf_op jit(solution)/shard_map/reduce-window
  10.7 0.8 slice_reduce_fusion
  11.8 1.1 fusion.25
  12.9 0.7 compare_select_fusion.1
  13.7 0.8 add_bitcast_fusion
  14.4 0.6 copy.15
  15.1 14.3 %scatter_custom_fusion = s32[2,16384]{0,1:T(8,128)} fusion(s32[4096]{0:T(1024)S(1)} %bitcast.88, s32[4096,2]{1,0:T(8,128)S(1)} %copy.15, s32[]{:T(128)} %constant.80.clone.1), kind=kCustom, calls=%fused_computation.20 | custom fusion | bytes 131076 | tf_op jit(solution)/shard_map/scatter | solution.py:101
  29.4 5.2 %copy.16 = s32[2,8,4,512]{3,2,0,1:T(4,128)S(1)} copy(s32[2,8,4,512]{0,3,2,1:T(8,128)} %bitcast.64) | data formatting | bytes 262144 | tf_op jit(solution)/shard_map/reshape | solution.py:119
  34.6 9.9 %all_to_all.20 = s32[2,8,4,512]{3,2,0,1:T(4,128)S(1)} all-to-all(s32[2,8,4,512]{3,2,0,1:T(4,128)S(1)} %copy.16), channel_id=1, replica_groups=mesh['gx'=8,'gy'=4] {'gx'}, dimensions={1} | all-to-all | bytes 262144 | tf_op jit(solution)/shard_map/all_to_all | solution.py:118
  44.5 0.7 copy.17
  45.3 5.3 %all-to-all-start.1 = ((s32[2,8,4,512]{3,1,0,2:T(8,128)}), s32[2,8,4,512]{3,1,0,2:T(8,128)S(1)}, u32[]{:S(2)}, u32[]{:S(2)}) async-start(s32[2,8,4,512]{3,1,0,2:T(8,128)} %copy.17), calls=%async_computation.1 | async-start | bytes 262144 | tf_op jit(solution)/shard_map/all_to_all | solution.py:117
  51.2 14.3 %scatter_custom_fusion.1 = f32[16,16384]{0,1:T(8,128)} fusion(s32[4096]{0:T(1024)S(1)} %bitcast.89, f32[4096,16]{1,0:T(8,128)S(1)} %copy.19, f32[]{:T(128)} %constant.79.clone.1), kind=kCustom, calls=%fused_computation.18 | custom fusion | bytes 1048580 | tf_op jit(solution)/shard_map/scatter | solution.py:99
  65.5 6.0 %copy.20 = f32[16,8,4,512]{3,2,0,1:T(4,128)} copy(f32[16,8,4,512]{0,3,2,1:T(8,128)} %bitcast.65) | data formatting | bytes 2097152 | tf_op jit(solution)/shard_map/reshape | solution.py:106
  71.6 5.3 %all-to-all-start.2 = ((f32[16,8,4,512]{3,2,0,1:T(4,128)}), f32[16,8,4,512]{3,2,0,1:T(4,128)S(1)}, u32[]{:S(2)}, u32[]{:S(2)}) async-start(f32[16,8,4,512]{3,2,0,1:T(4,128)} %copy.20), calls=%async_computation.2 | async-start | bytes 2097152 | tf_op jit(solution)/shard_map/all_to_all | solution.py:105
  77.2 23.9 %all-to-all-done.2 = f32[16,8,4,512]{3,2,0,1:T(4,128)S(1)} async-done(((f32[16,8,4,512]{3,2,0,1:T(4,128)}), f32[16,8,4,512]{3,2,0,1:T(4,128)S(1)}, u32[]{:S(2)}, u32[]{:S(2)}) %all-to-all-start.2) | async-done | bytes 1048608 | tf_op jit(solution)/shard_map/all_to_all | solution.py:105
  101.0 1.6 copy.21
  102.6 3.9 %all-to-all-start.3 = ((f32[16,8,4,512]{3,1,0,2:T(8,128)}), f32[16,8,4,512]{3,1,0,2:T(8,128)S(1)}, u32[]{:S(2)}, u32[]{:S(2)}) async-start(f32[16,8,4,512]{3,1,0,2:T(8,128)} %copy.21), calls=%async_computation.3 | async-start | bytes 2097152 | tf_op jit(solution)/shard_map/all_to_all | solution.py:104
  106.5 75.1 %while.28 = (s32[]{:T(128)}, f32[5,16384]{1,0:T(8,128)S(1)}, f32[5,4096]{1,0:T(8,128)S(1)}, s32[16384]{0:T(1024)S(1)}, s32[]{:T(128)}, /*index=5*/s32[]{:T(128)}, s32[]{:T(128)}, s32[]{:T(128)}) while((s32[]{:T(128)}, f32[5,16384]{1,0:T(8,128)S(1)}, f32[5,4096]{1,0:T(8,128)S(1)}, s32[16384]{0:T(1024)S(1)}, s32[]{:T(128)}, ...), condition=%wide.region_6.7_spmd.clone, body=%wide.region_5.6_spmd.clone.sunk | while | flops 511869440 | bytes 938141 | solution.py:60
  106.5 9.4 %fusion.54 = f32[5,16384]{1,0:T(8,128)S(1)} fusion(s32[16384]{0:T(1024)S(1)} %get-tuple-element.276, s32[512]{0:T(512)S(1)} %iota_add_fusion.5, f32[5,16384]{1,0:T(8,128)S(1)} %get-tuple-element.266, pred[]{:T(512)S(6)} %compare.3, f32[5,4096]{1,0:T(8,128)S(1)} %get-tuple-element.275, s32[]{:T(128)S(6)} %select_n.38), kind=kOutput, calls=%fused_computation.11.clone.1 | convolution fusion | flops 511868928 | bytes 935941 | tf_op jit(solution)/shard_map/while/body/eval_jaxpr/dot_general | solution.py:53
  115.9 9.4 %fusion.54 = f32[5,16384]{1,0:T(8,128)S(1)} fusion(s32[16384]{0:T(1024)S(1)} %get-tuple-element.276, s32[512]{0:T(512)S(1)} %iota_add_fusion.5, f32[5,16384]{1,0:T(8,128)S(1)} %get-tuple-element.266, pred[]{:T(512)S(6)} %compare.3, f32[5,4096]{1,0:T(8,128)S(1)} %get-tuple-element.275, s32[]{:T(128)S(6)} %select_n.38), kind=kOutput, calls=%fused_computation.11.clone.1 | convolution fusion | flops 511868928 | bytes 935941 | tf_op jit(solution)/shard_map/while/body/eval_jaxpr/dot_general | solution.py:53
  125.3 9.4 %fusion.54 = f32[5,16384]{1,0:T(8,128)S(1)} fusion(s32[16384]{0:T(1024)S(1)} %get-tuple-element.276, s32[512]{0:T(512)S(1)} %iota_add_fusion.5, f32[5,16384]{1,0:T(8,128)S(1)} %get-tuple-element.266, pred[]{:T(512)S(6)} %compare.3, f32[5,4096]{1,0:T(8,128)S(1)} %get-tuple-element.275, s32[]{:T(128)S(6)} %select_n.38), kind=kOutput, calls=%fused_computation.11.clone.1 | convolution fusion | flops 511868928 | bytes 935941 | tf_op jit(solution)/shard_map/while/body/eval_jaxpr/dot_general | solution.py:53
  134.7 9.4 %fusion.54 = f32[5,16384]{1,0:T(8,128)S(1)} fusion(s32[16384]{0:T(1024)S(1)} %get-tuple-element.276, s32[512]{0:T(512)S(1)} %iota_add_fusion.5, f32[5,16384]{1,0:T(8,128)S(1)} %get-tuple-element.266, pred[]{:T(512)S(6)} %compare.3, f32[5,4096]{1,0:T(8,128)S(1)} %get-tuple-element.275, s32[]{:T(128)S(6)} %select_n.38), kind=kOutput, calls=%fused_computation.11.clone.1 | convolution fusion | flops 511868928 | bytes 935941 | tf_op jit(solution)/shard_map/while/body/eval_jaxpr/dot_general | solution.py:53
  144.1 9.4 %fusion.54 = f32[5,16384]{1,0:T(8,128)S(1)} fusion(s32[16384]{0:T(1024)S(1)} %get-tuple-element.276, s32[512]{0:T(512)S(1)} %iota_add_fusion.5, f32[5,16384]{1,0:T(8,128)S(1)} %get-tuple-element.266, pred[]{:T(512)S(6)} %compare.3, f32[5,4096]{1,0:T(8,128)S(1)} %get-tuple-element.275, s32[]{:T(128)S(6)} %select_n.38), kind=kOutput, calls=%fused_computation.11.clone.1 | convolution fusion | flops 511868928 | bytes 935941 | tf_op jit(solution)/shard_map/while/body/eval_jaxpr/dot_general | solution.py:53
  153.5 9.4 %fusion.54 = f32[5,16384]{1,0:T(8,128)S(1)} fusion(s32[16384]{0:T(1024)S(1)} %get-tuple-element.276, s32[512]{0:T(512)S(1)} %iota_add_fusion.5, f32[5,16384]{1,0:T(8,128)S(1)} %get-tuple-element.266, pred[]{:T(512)S(6)} %compare.3, f32[5,4096]{1,0:T(8,128)S(1)} %get-tuple-element.275, s32[]{:T(128)S(6)} %select_n.38), kind=kOutput, calls=%fused_computation.11.clone.1 | convolution fusion | flops 511868928 | bytes 935941 | tf_op jit(solution)/shard_map/while/body/eval_jaxpr/dot_general | solution.py:53
  162.8 9.4 %fusion.54 = f32[5,16384]{1,0:T(8,128)S(1)} fusion(s32[16384]{0:T(1024)S(1)} %get-tuple-element.276, s32[512]{0:T(512)S(1)} %iota_add_fusion.5, f32[5,16384]{1,0:T(8,128)S(1)} %get-tuple-element.266, pred[]{:T(512)S(6)} %compare.3, f32[5,4096]{1,0:T(8,128)S(1)} %get-tuple-element.275, s32[]{:T(128)S(6)} %select_n.38), kind=kOutput, calls=%fused_computation.11.clone.1 | convolution fusion | flops 511868928 | bytes 935941 | tf_op jit(solution)/shard_map/while/body/eval_jaxpr/dot_general | solution.py:53
  172.2 9.4 %fusion.54 = f32[5,16384]{1,0:T(8,128)S(1)} fusion(s32[16384]{0:T(1024)S(1)} %get-tuple-element.276, s32[512]{0:T(512)S(1)} %iota_add_fusion.5, f32[5,16384]{1,0:T(8,128)S(1)} %get-tuple-element.266, pred[]{:T(512)S(6)} %compare.3, f32[5,4096]{1,0:T(8,128)S(1)} %get-tuple-element.275, s32[]{:T(128)S(6)} %select_n.38), kind=kOutput, calls=%fused_computation.11.clone.1 | convolution fusion | flops 511868928 | bytes 935941 | tf_op jit(solution)/shard_map/while/body/eval_jaxpr/dot_general | solution.py:53
  183.3 1.3 copy.27
  184.6 1.6 slice.110
  186.7 1.3 multiply_reduce_fusion
  188.3 1.8 add_multiply_fusion
  190.2 1.3 fusion.28
  191.6 110.3 %while.27 = (s32[]{:T(128)}, f32[5,4096]{1,0:T(8,128)S(1)}, s32[1,16384]{1,0:T(1,128)S(1)}, f32[5,16384]{1,0:T(8,128)S(1)}, s32[]{:T(128)}, /*index=5*/s32[]{:T(128)}, s32[]{:T(128)}, s32[]{:T(128)}) while((s32[]{:T(128)}, f32[5,4096]{1,0:T(8,128)S(1)}, s32[1,16384]{1,0:T(1,128)S(1)}, f32[5,16384]{1,0:T(8,128)S(1)}, s32[]{:T(128)}, ...), condition=%wide.region_10.11_spmd, body=%wide.region_9.10_spmd.sunk | while | flops 511705600 | bytes 610451 | solution.py:79
  191.9 13.7 %fusion.51 = f32[5,4096]{1,0:T(8,128)S(1)} fusion(f32[5,4096]{1,0:T(8,128)S(1)} %get-tuple-element.290, s32[]{:T(128)S(6)} %select_n.37, f32[5,16384]{1,0:T(8,128)S(1)} %get-tuple-element.300, s32[16384]{0:T(1024)S(1)} %bitcast.85, s32[512]{0:T(512)S(1)} %iota_add_fusion.4), kind=kOutput, calls=%fused_computation.7.clone.1 | convolution fusion | flops 511705088 | bytes 608260 | tf_op jit(solution)/shard_map/while/body/eval_jaxpr/dot_general | solution.py:70
  205.6 13.8 %fusion.51 = f32[5,4096]{1,0:T(8,128)S(1)} fusion(f32[5,4096]{1,0:T(8,128)S(1)} %get-tuple-element.290, s32[]{:T(128)S(6)} %select_n.37, f32[5,16384]{1,0:T(8,128)S(1)} %get-tuple-element.300, s32[16384]{0:T(1024)S(1)} %bitcast.85, s32[512]{0:T(512)S(1)} %iota_add_fusion.4), kind=kOutput, calls=%fused_computation.7.clone.1 | convolution fusion | flops 511705088 | bytes 608260 | tf_op jit(solution)/shard_map/while/body/eval_jaxpr/dot_general | solution.py:70
  219.4 13.8 %fusion.51 = f32[5,4096]{1,0:T(8,128)S(1)} fusion(f32[5,4096]{1,0:T(8,128)S(1)} %get-tuple-element.290, s32[]{:T(128)S(6)} %select_n.37, f32[5,16384]{1,0:T(8,128)S(1)} %get-tuple-element.300, s32[16384]{0:T(1024)S(1)} %bitcast.85, s32[512]{0:T(512)S(1)} %iota_add_fusion.4), kind=kOutput, calls=%fused_computation.7.clone.1 | convolution fusion | flops 511705088 | bytes 608260 | tf_op jit(solution)/shard_map/while/body/eval_jaxpr/dot_general | solution.py:70
  233.2 13.8 %fusion.51 = f32[5,4096]{1,0:T(8,128)S(1)} fusion(f32[5,4096]{1,0:T(8,128)S(1)} %get-tuple-element.290, s32[]{:T(128)S(6)} %select_n.37, f32[5,16384]{1,0:T(8,128)S(1)} %get-tuple-element.300, s32[16384]{0:T(1024)S(1)} %bitcast.85, s32[512]{0:T(512)S(1)} %iota_add_fusion.4), kind=kOutput, calls=%fused_computation.7.clone.1 | convolution fusion | flops 511705088 | bytes 608260 | tf_op jit(solution)/shard_map/while/body/eval_jaxpr/dot_general | solution.py:70
  246.9 13.8 %fusion.51 = f32[5,4096]{1,0:T(8,128)S(1)} fusion(f32[5,4096]{1,0:T(8,128)S(1)} %get-tuple-element.290, s32[]{:T(128)S(6)} %select_n.37, f32[5,16384]{1,0:T(8,128)S(1)} %get-tuple-element.300, s32[16384]{0:T(1024)S(1)} %bitcast.85, s32[512]{0:T(512)S(1)} %iota_add_fusion.4), kind=kOutput, calls=%fused_computation.7.clone.1 | convolution fusion | flops 511705088 | bytes 608260 | tf_op jit(solution)/shard_map/while/body/eval_jaxpr/dot_general | solution.py:70
  260.7 13.8 %fusion.51 = f32[5,4096]{1,0:T(8,128)S(1)} fusion(f32[5,4096]{1,0:T(8,128)S(1)} %get-tuple-element.290, s32[]{:T(128)S(6)} %select_n.37, f32[5,16384]{1,0:T(8,128)S(1)} %get-tuple-element.300, s32[16384]{0:T(1024)S(1)} %bitcast.85, s32[512]{0:T(512)S(1)} %iota_add_fusion.4), kind=kOutput, calls=%fused_computation.7.clone.1 | convolution fusion | flops 511705088 | bytes 608260 | tf_op jit(solution)/shard_map/while/body/eval_jaxpr/dot_general | solution.py:70
  274.5 13.8 %fusion.51 = f32[5,4096]{1,0:T(8,128)S(1)} fusion(f32[5,4096]{1,0:T(8,128)S(1)} %get-tuple-element.290, s32[]{:T(128)S(6)} %select_n.37, f32[5,16384]{1,0:T(8,128)S(1)} %get-tuple-element.300, s32[16384]{0:T(1024)S(1)} %bitcast.85, s32[512]{0:T(512)S(1)} %iota_add_fusion.4), kind=kOutput, calls=%fused_computation.7.clone.1 | convolution fusion | flops 511705088 | bytes 608260 | tf_op jit(solution)/shard_map/while/body/eval_jaxpr/dot_general | solution.py:70
  288.2 13.8 %fusion.51 = f32[5,4096]{1,0:T(8,128)S(1)} fusion(f32[5,4096]{1,0:T(8,128)S(1)} %get-tuple-element.290, s32[]{:T(128)S(6)} %select_n.37, f32[5,16384]{1,0:T(8,128)S(1)} %get-tuple-element.300, s32[16384]{0:T(1024)S(1)} %bitcast.85, s32[512]{0:T(512)S(1)} %iota_add_fusion.4), kind=kOutput, calls=%fused_computation.7.clone.1 | convolution fusion | flops 511705088 | bytes 608260 | tf_op jit(solution)/shard_map/while/body/eval_jaxpr/dot_general | solution.py:70
  302.0 4.9 %collective-permute-start = (f32[5,1,128]{2,1,0:T(1,128)S(1)}, f32[5,1,128]{2,1,0:T(1,128)S(1)}, u32[]{:S(2)}, u32[]{:S(2)}) collective-permute-start(f32[5,1,128]{2,1,0:T(1,128)S(1)} %get-tuple-element.204), channel_id=1, source_target_pairs={{4,0},{8,4},{12,8},{16,12},{20,16},{24,20},{28,24},{5,1},{9,5},{13... | collective-permute-start | bytes 7688 | tf_op jit(solution)/shard_map/ppermute | solution.py:16
  307.0 1.9 collective-permute-start.1
  308.9 3.3 %collective-permute-done.1 = f32[5,1,128]{2,1,0:T(1,128)S(1)} collective-permute-done((f32[5,1,128]{2,1,0:T(1,128)S(1)}, f32[5,1,128]{2,1,0:T(1,128)S(1)}, u32[]{:S(2)}, u32[]{:S(2)}) %collective-permute-start.1) | collective-permute-done | bytes 2592 | tf_op jit(solution)/shard_map/ppermute | solution.py:15
  312.3 5.0 %collective-permute-start.3 = (f32[5,34,1]{2,1,0:T(8,128)S(1)}, f32[5,34,1]{2,1,0:T(8,128)S(1)}, u32[]{:S(2)}, u32[]{:S(2)}) collective-permute-start(f32[5,34,1]{2,1,0:T(8,128)S(1)} %get-tuple-element.202), channel_id=1, source_target_pairs={{0,1},{1,2},{2,3},{4,5},{5,6},{6,7},{8,9},{9,10},{10,11},{12,13},{... | collective-permute-start | bytes 2048 | tf_op jit(solution)/shard_map/ppermute | solution.py:15
  317.3 1.9 collective-permute-start.2
  319.2 4.0 %collective-permute-done.2 = f32[5,34,1]{2,1,0:T(8,128)S(1)} collective-permute-done((f32[5,34,1]{2,1,0:T(8,128)S(1)}, f32[5,34,1]{2,1,0:T(8,128)S(1)}, u32[]{:S(2)}, u32[]{:S(2)}) %collective-permute-start.2) | collective-permute-done | bytes 712 | tf_op jit(solution)/shard_map/ppermute | solution.py:16
  324.1 0.6 slice_add_fusion
  (66 shorter events, 4.7 us)
Async XLA Ops:
  0.6 181.8 %copy-start = (f32[8,16]{1,0:T(8,128)S(1)}, f32[8,16]{1,0:T(8,128)}, u32[]{:S(2)}) copy-start(f32[8,16]{1,0:T(8,128)} %param.15) | copy-start | bytes 1540
  15.1 35.5 %copy-start.2 = (f32[16,4096]{1,0:T(8,128)S(1)}, f32[16,4096]{1,0:T(8,128)}, u32[]{:S(2)}) copy-start(f32[16,4096]{1,0:T(8,128)} %param.11) | copy-start | bytes 786436
  45.3 26.3 %all-to-all-start.1 = ((s32[2,8,4,512]{3,1,0,2:T(8,128)}), s32[2,8,4,512]{3,1,0,2:T(8,128)S(1)}, u32[]{:S(2)}, u32[]{:S(2)}) async-start(s32[2,8,4,512]{3,1,0,2:T(8,128)} %copy.17), calls=%async_computation.1 | async-start | bytes 262144 | tf_op jit(solution)/shard_map/all_to_all | solution.py:117
  51.2 25.7 %copy-start.3 = (f32[4,32,128]{2,1,0:T(8,128)S(1)}, f32[4,32,128]{2,1,0:T(8,128)}, u32[]{:S(2)}) copy-start(f32[4,32,128]{2,1,0:T(8,128)} %param.17) | copy-start | bytes 196612
  51.2 25.8 %copy-start.4 = (f32[32,128]{1,0:T(8,128)S(1)}, f32[32,128]{1,0:T(8,128)}, u32[]{:S(2)}) copy-start(f32[32,128]{1,0:T(8,128)} %param.16) | copy-start | bytes 49156
  71.6 29.5 %all-to-all-start.2 = ((f32[16,8,4,512]{3,2,0,1:T(4,128)}), f32[16,8,4,512]{3,2,0,1:T(4,128)S(1)}, u32[]{:S(2)}, u32[]{:S(2)}) async-start(f32[16,8,4,512]{3,2,0,1:T(4,128)} %copy.20), calls=%async_computation.2 | async-start | bytes 2097152 | tf_op jit(solution)/shard_map/all_to_all | solution.py:105
  102.6 80.4 %all-to-all-start.3 = ((f32[16,8,4,512]{3,1,0,2:T(8,128)}), f32[16,8,4,512]{3,1,0,2:T(8,128)S(1)}, u32[]{:S(2)}, u32[]{:S(2)}) async-start(f32[16,8,4,512]{3,1,0,2:T(8,128)} %copy.21), calls=%async_computation.3 | async-start | bytes 2097152 | tf_op jit(solution)/shard_map/all_to_all | solution.py:104
  181.6 0.8 copy-start.1
  191.6 131.8 %copy-start.5 = (f32[32,128]{1,0:T(8,128)S(1)}, f32[32,128]{1,0:T(8,128)}, u32[]{:S(2)}) copy-start(f32[32,128]{1,0:T(8,128)} %param.16) | copy-start | bytes 49156
  302.0 6.9 %collective-permute-start = (f32[5,1,128]{2,1,0:T(1,128)S(1)}, f32[5,1,128]{2,1,0:T(1,128)S(1)}, u32[]{:S(2)}, u32[]{:S(2)}) collective-permute-start(f32[5,1,128]{2,1,0:T(1,128)S(1)} %get-tuple-element.204), channel_id=1, source_target_pairs={{4,0},{8,4},{12,8},{16,12},{20,16},{24,20},{28,24},{5,1},{9,5},{13... | collective-permute-start | bytes 7688 | tf_op jit(solution)/shard_map/ppermute | solution.py:16
  307.0 5.2 %collective-permute-start.1 = (f32[5,1,128]{2,1,0:T(1,128)S(1)}, f32[5,1,128]{2,1,0:T(1,128)S(1)}, u32[]{:S(2)}, u32[]{:S(2)}) collective-permute-start(f32[5,1,128]{2,1,0:T(1,128)S(1)} %get-tuple-element.203), channel_id=1, source_target_pairs={{0,4},{4,8},{8,12},{12,16},{16,20},{20,24},{24,28},{1,5},{5,9},{9,... | collective-permute-start | bytes 7688 | tf_op jit(solution)/shard_map/ppermute | solution.py:15
  312.3 6.9 %collective-permute-start.3 = (f32[5,34,1]{2,1,0:T(8,128)S(1)}, f32[5,34,1]{2,1,0:T(8,128)S(1)}, u32[]{:S(2)}, u32[]{:S(2)}) collective-permute-start(f32[5,34,1]{2,1,0:T(8,128)S(1)} %get-tuple-element.202), channel_id=1, source_target_pairs={{0,1},{1,2},{2,3},{4,5},{5,6},{6,7},{8,9},{9,10},{10,11},{12,13},{... | collective-permute-start | bytes 2048 | tf_op jit(solution)/shard_map/ppermute | solution.py:15
  317.3 6.0 %collective-permute-start.2 = (f32[5,34,1]{2,1,0:T(8,128)S(1)}, f32[5,34,1]{2,1,0:T(8,128)S(1)}, u32[]{:S(2)}, u32[]{:S(2)}) collective-permute-start(f32[5,34,1]{2,1,0:T(8,128)S(1)} %get-tuple-element.201), channel_id=1, source_target_pairs={{1,0},{2,1},{3,2},{5,4},{6,5},{7,6},{9,8},{10,9},{11,10},{13,12},{... | collective-permute-start | bytes 2048 | tf_op jit(solution)/shard_map/ppermute | solution.py:16
where the time goes:
time: 326 us; the launch traced here: 325 us
  matrix products  186 us (57%)
  local copies, waits for them, and re-layouts  48.9 us (15%)
  waiting for transfers between devices  31.2 us (10%)
  starting transfers between devices  28.3 us (9%)
  other arithmetic  19.4 us (6%)
  blocking collectives  9.88 us (3%)
    dot_general x8, matrix products, deposit_advance(): lax.dot_general(source, cell_hot(cells, first, width), (((1,), (1,)), (()...  110 us
    dot_general x8, matrix products, look_advance(): jnp.dot(block, cell_hot(cells, first, width), precision=lax.Precision.HIG...  75 us
    all_to_all x1, waiting for transfers between devices, per_device(): lax.all_to_all(float_buf.reshape(-1, width_x, width_y, capacity), 'gx', s...  23.9 us
    scatter x1, local copies, waits for them, and re-layouts, per_device(): jnp.full((2, slots), -1, jnp.int32).at[:, slot]  14.3 us
    scatter x1, local copies, waits for them, and re-layouts, per_device(): jnp.zeros((parcel_props.shape[0], slots), jnp.float32).at[:, slot]  14.3 us
    all_to_all x1, blocking collectives, per_device(): lax.all_to_all(int_buf.reshape(2, width_x, width_y, capacity), 'gx', spli...  9.88 us
    another operation x3, other arithmetic  9.62 us
    ppermute x2, starting transfers between devices, with_halo(): before = lax.ppermute(last, axis, up)  6.89 us
  transfers between devices with their start and end apart: 7, of which 3 were waited for; matrix products, arithmetic and copies ran while one was open for 30% of the time, Pallas kernels for 0%

commit v1 on v0

--- a/solution.py
+++ b/solution.py
@@ -3,6 +3,14 @@
 import jax.numpy as jnp
 from jax import lax
 from jax.sharding import PartitionSpec as P
+
+
+def use_inputs_on_mesh(field_in, link_axis="gx"):
+    x_new = jax.lax.axis_size(link_axis)
+    b_next = jnp.split(field_in, x_new, axis=1)
+    tall = jnp.stack(b_next, axis=0)
+    x_next = jax.lax.all_to_all(tall, axis_name=link_axis, split_axis=0, concat_axis=0)
+    return jnp.concatenate(x_next, axis=1)
 
 
 def with_halo(shard, sides, width):
@@ -102,13 +110,7 @@
     )
     got_floats, got_ints = (
         lax.all_to_all(
-            lax.all_to_all(
-                float_buf.reshape(-1, width_x, width_y, capacity),
-                "gx",
-                split_axis=1,
-                concat_axis=1,
-                tiled=True,
-            ),
+            use_inputs_on_mesh(float_buf.reshape(-1, width_x, width_y, capacity)),
             "gy",
             split_axis=2,
             concat_axis=2,

time: 326 us -> 347 us (1.064)
  local copies, waits for them, and re-layouts: 48.9 us -> 68.1 us
  blocking collectives: 9.88 us -> 0 us
  starting transfers between devices: 28.3 us -> 34.8 us
  matrix products: 186 us -> 192 us
    unnamed x18 -> x31, local copies, waits for them, and re-layouts: 1.4 us -> 18 us
    all_to_all x1 -> x0, blocking collectives: 9.88 us -> none  [per_device(): lax.all_to_all(int_buf.reshape(2, width_x, width_y, capacity), 'gx', spli...]
    all_to_all x2 -> x3, starting transfers between devices: 9.27 us -> 16.6 us  [the longest x1 5.69 us: per_device(): lax.all_to_all(int_buf.reshape(2, width_x, width_y, capacity), 'gx', spli...]
    dot_general x8, matrix products: 110 us -> 117 us  [deposit_advance(): lax.dot_general(source, cell_hot(cells, first, width), (((1,), (1,)), (()...]
    split x0 -> x1, local copies, waits for them, and re-layouts: none -> 5.82 us  [use_inputs_on_mesh(): b_next = jnp.split(field_in, x_new, axis=1)]
    reshape x1, local copies, waits for them, and re-layouts: 6.02 us -> 1.58 us  [use_inputs_on_mesh(): return jnp.concatenate(x_next, axis=1)]
    ppermute x2, waiting for transfers between devices: 4.04 us -> 0.4 us  [with_halo(): after = lax.ppermute(leading, axis, down)]
    all_to_all x2 -> x3, waiting for transfers between devices: 23.9 us -> 20.9 us  [the longest x1 20.8 us: use_inputs_on_mesh(): jax.lax.all_to_all(tall, axis_name=link_axis, split_axis=0, concat_axis=0)]
  transfers between devices with their start and end apart: 7 -> 8, of which waited for: 3 -> 5; matrix products, arithmetic and copies ran while one was open for 30% -> 34% of each run, Pallas kernels for 0% -> 0%
where the time goes in v1:
time: 347 us; the launch traced here: 345 us
  matrix products  192 us (55%)
  local copies, waits for them, and re-layouts  68.1 us (20%)
  starting transfers between devices  34.8 us (10%)
  waiting for transfers between devices  28.7 us (8%)
  other arithmetic  19.7 us (6%)
    dot_general x8, matrix products, deposit_advance(): lax.dot_general(source, cell_hot(cells, first, width), (((1,), (1,)), (()...  117 us
    dot_general x8, matrix products, look_advance(): jnp.dot(block, cell_hot(cells, first, width), precision=lax.Precision.HIG...  75 us
    all_to_all x1, waiting for transfers between devices, use_inputs_on_mesh(): jax.lax.all_to_all(tall, axis_name=link_axis, split_axis=0, concat_axis=0)  20.8 us
    unnamed x31, local copies, waits for them, and re-layouts  18 us
    scatter x1, local copies, waits for them, and re-layouts, per_device(): jnp.zeros((parcel_props.shape[0], slots), jnp.float32).at[:, slot]  14.3 us
    scatter x1, local copies, waits for them, and re-layouts, per_device(): jnp.full((2, slots), -1, jnp.int32).at[:, slot]  14.3 us
    another operation x3, other arithmetic  9.62 us
    ppermute x2, starting transfers between devices, with_halo(): after = lax.ppermute(leading, axis, down)  8.49 us
  transfers between devices with their start and end apart: 8, of which 5 were waited for; matrix products, arithmetic and copies ran while one was open for 34% of the time, Pallas kernels for 0%

profile of v1, /device:TPU:9, one launch (start us, length us, event | category | flops | bytes accessed | tf_op | source)
XLA Modules:
  0.0 344.9 jit_solution(5918385319247240529)
XLA Ops:
  1.4 9.2 %reduce-window.6 = s32[32,32,128]{2,1,0:T(8,128)S(1)} reduce-window(s32[32,32,128]{2,1,0:T(8,128)S(1)} %fusion.26, s32[]{:T(128)} %constant.78.clone.1), window={size=1x1x128 pad=0_0x0_0x127_0}, to_apply=%region_0.0 | reduce-window | flops 16646144 | bytes 1048580 | tf_op jit(solution)/shard_map/reduce-window
  15.1 14.3 %scatter_custom_fusion = s32[2,16384]{0,1:T(8,128)} fusion(s32[4096]{0:T(1024)S(1)} %bitcast.108, s32[4096,2]{1,0:T(8,128)S(1)} %copy.29, s32[]{:T(128)} %constant.80.clone.1), kind=kCustom, calls=%fused_computation.20 | custom fusion | bytes 131076 | tf_op jit(solution)/shard_map/scatter | solution.py:109
  29.4 5.8 %copy.30 = s32[2,8,4,512]{3,2,0,1:T(4,128)} copy(s32[2,8,4,512]{0,3,2,1:T(8,128)} %bitcast.84) | data formatting | bytes 262144 | tf_op jit(solution)/shard_map/reshape | solution.py:121
  35.3 5.7 %all-to-all-start = ((s32[2,8,4,512]{3,2,0,1:T(4,128)}), s32[2,8,4,512]{3,2,0,1:T(4,128)}, u32[]{:S(2)}, u32[]{:S(2)}) async-start(s32[2,8,4,512]{3,2,0,1:T(4,128)} %copy.30), calls=%async_computation | async-start | bytes 262144 | tf_op jit(solution)/shard_map/all_to_all | solution.py:120
  41.6 14.3 %scatter_custom_fusion.1 = f32[16,16384]{0,1:T(8,128)} fusion(s32[4096]{0:T(1024)S(1)} %bitcast.109, f32[4096,16]{1,0:T(8,128)S(1)} %copy.33, f32[]{:T(128)} %constant.79.clone.1), kind=kCustom, calls=%fused_computation.18 | custom fusion | bytes 1048580 | tf_op jit(solution)/shard_map/scatter | solution.py:107
  55.9 5.8 %fusion.39 = (f32[16,1,4,512]{0,3,2,1:T(8,128)S(1)}, f32[16,1,4,512]{0,3,2,1:T(8,128)S(1)}, f32[16,1,4,512]{0,3,2,1:T(8,128)S(1)}, f32[16,1,4,512]{0,3,2,1:T(8,1...) fusion(f32[16,8,4,512]{0,3,2,1:T(8,128)} %bitcast.83), kind=kLoop, calls=%fused_computation.84 | loop fusion | bytes 2097152 | tf_op jit(solution)/shard_map/split | solution.py:10
  61.7 1.5 copy.49
  63.9 2.2 copy.50
  66.1 2.2 copy.51
  68.3 1.5 copy.52
  69.8 1.5 copy.53
  72.3 1.6 bitcast_dynamic-update-slice_fusion.6
  73.9 1.6 bitcast_dynamic-update-slice_fusion.5
  78.1 1.6 copy.31
  79.7 4.5 %all-to-all-start.1 = ((s32[2,8,4,512]{3,1,0,2:T(8,128)}), s32[2,8,4,512]{3,1,0,2:T(8,128)S(1)}, u32[]{:S(2)}, u32[]{:S(2)}) async-start(s32[2,8,4,512]{3,1,0,2:T(8,128)} %copy.31), calls=%async_computation.1 | async-start | bytes 262144 | tf_op jit(solution)/shard_map/all_to_all | solution.py:119
  84.9 2.9 all-to-all-done.1
  87.8 5.4 %all-to-all-start.2 = ((f32[8,16,1,4,512]{4,3,1,2,0:T(4,128)}), f32[8,16,1,4,512]{4,3,1,2,0:T(4,128)S(1)}, u32[]{:S(2)}, u32[]{:S(2)}) async-start(f32[8,16,1,4,512]{4,3,1,2,0:T(4,128)} %bitcast_dynamic-update-slice_fusion), calls=%async_computation.2 | async-start | bytes 2097152 | tf_op jit(solution)/shard_map/all_to_all | solution.py:12
  95.0 20.8 %all-to-all-done.2 = f32[8,16,1,4,512]{4,3,1,2,0:T(4,128)S(1)} async-done(((f32[8,16,1,4,512]{4,3,1,2,0:T(4,128)}), f32[8,16,1,4,512]{4,3,1,2,0:T(4,128)S(1)}, u32[]{:S(2)}, u32[]{:S(2)}) %all-to-all-start.2) | async-done | bytes 1048608 | tf_op jit(solution)/shard_map/all_to_all | solution.py:12
  115.9 1.6 copy.42
  117.5 5.4 %all-to-all-start.3 = ((f32[16,8,4,512]{3,1,0,2:T(8,128)}), f32[16,8,4,512]{3,1,0,2:T(8,128)S(1)}, u32[]{:S(2)}, u32[]{:S(2)}) async-start(f32[16,8,4,512]{3,1,0,2:T(8,128)} %copy.42), calls=%async_computation.3 | async-start | bytes 2097152 | tf_op jit(solution)/shard_map/all_to_all | solution.py:112
  122.9 75.1 %while.28 = (s32[]{:T(128)}, f32[5,16384]{1,0:T(8,128)S(1)}, f32[5,4096]{1,0:T(8,128)S(1)}, s32[16384]{0:T(1024)S(1)}, s32[]{:T(128)}, /*index=5*/s32[]{:T(128)}, s32[]{:T(128)}, s32[]{:T(128)}) while((s32[]{:T(128)}, f32[5,16384]{1,0:T(8,128)S(1)}, f32[5,4096]{1,0:T(8,128)S(1)}, s32[16384]{0:T(1024)S(1)}, s32[]{:T(128)}, ...), condition=%wide.region_6.7_spmd.clone, body=%wide.region_5.6_spmd.clone.sunk | while | flops 511869440 | bytes 938133 | solution.py:68
  122.9 9.4 %fusion.55 = f32[5,16384]{1,0:T(8,128)S(1)} fusion(s32[16384]{0:T(1024)S(1)} %get-tuple-element.284, s32[512]{0:T(512)S(1)} %iota_add_fusion.5, f32[5,16384]{1,0:T(8,128)S(1)} %get-tuple-element.274, pred[]{:T(512)S(6)} %compare.3, f32[5,4096]{1,0:T(8,128)S(1)} %get-tuple-element.283, s32[]{:T(128)S(6)} %select_n.38), kind=kOutput, calls=%fused_computation.11.clone.1 | convolution fusion | flops 511868928 | bytes 935941 | tf_op jit(solution)/shard_map/while/body/eval_jaxpr/dot_general | solution.py:61
  132.3 9.4 %fusion.55 = f32[5,16384]{1,0:T(8,128)S(1)} fusion(s32[16384]{0:T(1024)S(1)} %get-tuple-element.284, s32[512]{0:T(512)S(1)} %iota_add_fusion.5, f32[5,16384]{1,0:T(8,128)S(1)} %get-tuple-element.274, pred[]{:T(512)S(6)} %compare.3, f32[5,4096]{1,0:T(8,128)S(1)} %get-tuple-element.283, s32[]{:T(128)S(6)} %select_n.38), kind=kOutput, calls=%fused_computation.11.clone.1 | convolution fusion | flops 511868928 | bytes 935941 | tf_op jit(solution)/shard_map/while/body/eval_jaxpr/dot_general | solution.py:61
  141.7 9.4 %fusion.55 = f32[5,16384]{1,0:T(8,128)S(1)} fusion(s32[16384]{0:T(1024)S(1)} %get-tuple-element.284, s32[512]{0:T(512)S(1)} %iota_add_fusion.5, f32[5,16384]{1,0:T(8,128)S(1)} %get-tuple-element.274, pred[]{:T(512)S(6)} %compare.3, f32[5,4096]{1,0:T(8,128)S(1)} %get-tuple-element.283, s32[]{:T(128)S(6)} %select_n.38), kind=kOutput, calls=%fused_computation.11.clone.1 | convolution fusion | flops 511868928 | bytes 935941 | tf_op jit(solution)/shard_map/while/body/eval_jaxpr/dot_general | solution.py:61
  151.1 9.4 %fusion.55 = f32[5,16384]{1,0:T(8,128)S(1)} fusion(s32[16384]{0:T(1024)S(1)} %get-tuple-element.284, s32[512]{0:T(512)S(1)} %iota_add_fusion.5, f32[5,16384]{1,0:T(8,128)S(1)} %get-tuple-element.274, pred[]{:T(512)S(6)} %compare.3, f32[5,4096]{1,0:T(8,128)S(1)} %get-tuple-element.283, s32[]{:T(128)S(6)} %select_n.38), kind=kOutput, calls=%fused_computation.11.clone.1 | convolution fusion | flops 511868928 | bytes 935941 | tf_op jit(solution)/shard_map/while/body/eval_jaxpr/dot_general | solution.py:61
  160.4 9.4 %fusion.55 = f32[5,16384]{1,0:T(8,128)S(1)} fusion(s32[16384]{0:T(1024)S(1)} %get-tuple-element.284, s32[512]{0:T(512)S(1)} %iota_add_fusion.5, f32[5,16384]{1,0:T(8,128)S(1)} %get-tuple-element.274, pred[]{:T(512)S(6)} %compare.3, f32[5,4096]{1,0:T(8,128)S(1)} %get-tuple-element.283, s32[]{:T(128)S(6)} %select_n.38), kind=kOutput, calls=%fused_computation.11.clone.1 | convolution fusion | flops 511868928 | bytes 935941 | tf_op jit(solution)/shard_map/while/body/eval_jaxpr/dot_general | solution.py:61
  169.8 9.4 %fusion.55 = f32[5,16384]{1,0:T(8,128)S(1)} fusion(s32[16384]{0:T(1024)S(1)} %get-tuple-element.284, s32[512]{0:T(512)S(1)} %iota_add_fusion.5, f32[5,16384]{1,0:T(8,128)S(1)} %get-tuple-element.274, pred[]{:T(512)S(6)} %compare.3, f32[5,4096]{1,0:T(8,128)S(1)} %get-tuple-element.283, s32[]{:T(128)S(6)} %select_n.38), kind=kOutput, calls=%fused_computation.11.clone.1 | convolution fusion | flops 511868928 | bytes 935941 | tf_op jit(solution)/shard_map/while/body/eval_jaxpr/dot_general | solution.py:61
  179.2 9.4 %fusion.55 = f32[5,16384]{1,0:T(8,128)S(1)} fusion(s32[16384]{0:T(1024)S(1)} %get-tuple-element.284, s32[512]{0:T(512)S(1)} %iota_add_fusion.5, f32[5,16384]{1,0:T(8,128)S(1)} %get-tuple-element.274, pred[]{:T(512)S(6)} %compare.3, f32[5,4096]{1,0:T(8,128)S(1)} %get-tuple-element.283, s32[]{:T(128)S(6)} %select_n.38), kind=kOutput, calls=%fused_computation.11.clone.1 | convolution fusion | flops 511868928 | bytes 935941 | tf_op jit(solution)/shard_map/while/body/eval_jaxpr/dot_general | solution.py:61
  188.6 9.4 %fusion.55 = f32[5,16384]{1,0:T(8,128)S(1)} fusion(s32[16384]{0:T(1024)S(1)} %get-tuple-element.284, s32[512]{0:T(512)S(1)} %iota_add_fusion.5, f32[5,16384]{1,0:T(8,128)S(1)} %get-tuple-element.274, pred[]{:T(512)S(6)} %compare.3, f32[5,4096]{1,0:T(8,128)S(1)} %get-tuple-element.283, s32[]{:T(128)S(6)} %select_n.38), kind=kOutput, calls=%fused_computation.11.clone.1 | convolution fusion | flops 511868928 | bytes 935941 | tf_op jit(solution)/shard_map/while/body/eval_jaxpr/dot_general | solution.py:61
  200.8 1.3 copy.48
  202.1 1.6 slice.110
  204.3 1.8 add_multiply_fusion
  206.2 1.3 fusion.28
  207.7 116.9 %while.27 = (s32[]{:T(128)}, f32[5,4096]{1,0:T(8,128)S(1)}, s32[1,16384]{1,0:T(1,128)}, f32[5,16384]{1,0:T(8,128)S(1)}, s32[]{:T(128)}, /*index=5*/s32[]{:T(128)}, s32[]{:T(128)}, s32[]{:T(128)}) while((s32[]{:T(128)}, f32[5,4096]{1,0:T(8,128)S(1)}, s32[1,16384]{1,0:T(1,128)}, f32[5,16384]{1,0:T(8,128)S(1)}, s32[]{:T(128)}, ...), condition=%wide.region_10.11_spmd, body=%wide.region_9.10_spmd.sunk | while | flops 511705600 | bytes 610443 | solution.py:87
  207.9 14.6 %fusion.52 = f32[5,4096]{1,0:T(8,128)S(1)} fusion(f32[5,4096]{1,0:T(8,128)S(1)} %get-tuple-element.298, s32[]{:T(128)S(6)} %select_n.37, f32[5,16384]{1,0:T(8,128)S(1)} %get-tuple-element.308, s32[16384]{0:T(1024)} %bitcast.105, s32[512]{0:T(512)S(1)} %iota_add_fusion.4), kind=kOutput, calls=%fused_computation.7.clone.1 | convolution fusion | flops 511705088 | bytes 608260 | tf_op jit(solution)/shard_map/while/body/eval_jaxpr/dot_general | solution.py:78
  222.5 14.6 %fusion.52 = f32[5,4096]{1,0:T(8,128)S(1)} fusion(f32[5,4096]{1,0:T(8,128)S(1)} %get-tuple-element.298, s32[]{:T(128)S(6)} %select_n.37, f32[5,16384]{1,0:T(8,128)S(1)} %get-tuple-element.308, s32[16384]{0:T(1024)} %bitcast.105, s32[512]{0:T(512)S(1)} %iota_add_fusion.4), kind=kOutput, calls=%fused_computation.7.clone.1 | convolution fusion | flops 511705088 | bytes 608260 | tf_op jit(solution)/shard_map/while/body/eval_jaxpr/dot_general | solution.py:78
  237.1 14.6 %fusion.52 = f32[5,4096]{1,0:T(8,128)S(1)} fusion(f32[5,4096]{1,0:T(8,128)S(1)} %get-tuple-element.298, s32[]{:T(128)S(6)} %select_n.37, f32[5,16384]{1,0:T(8,128)S(1)} %get-tuple-element.308, s32[16384]{0:T(1024)} %bitcast.105, s32[512]{0:T(512)S(1)} %iota_add_fusion.4), kind=kOutput, calls=%fused_computation.7.clone.1 | convolution fusion | flops 511705088 | bytes 608260 | tf_op jit(solution)/shard_map/while/body/eval_jaxpr/dot_general | solution.py:78
  251.7 14.6 %fusion.52 = f32[5,4096]{1,0:T(8,128)S(1)} fusion(f32[5,4096]{1,0:T(8,128)S(1)} %get-tuple-element.298, s32[]{:T(128)S(6)} %select_n.37, f32[5,16384]{1,0:T(8,128)S(1)} %get-tuple-element.308, s32[16384]{0:T(1024)} %bitcast.105, s32[512]{0:T(512)S(1)} %iota_add_fusion.4), kind=kOutput, calls=%fused_computation.7.clone.1 | convolution fusion | flops 511705088 | bytes 608260 | tf_op jit(solution)/shard_map/while/body/eval_jaxpr/dot_general | solution.py:78
  266.3 14.6 %fusion.52 = f32[5,4096]{1,0:T(8,128)S(1)} fusion(f32[5,4096]{1,0:T(8,128)S(1)} %get-tuple-element.298, s32[]{:T(128)S(6)} %select_n.37, f32[5,16384]{1,0:T(8,128)S(1)} %get-tuple-element.308, s32[16384]{0:T(1024)} %bitcast.105, s32[512]{0:T(512)S(1)} %iota_add_fusion.4), kind=kOutput, calls=%fused_computation.7.clone.1 | convolution fusion | flops 511705088 | bytes 608260 | tf_op jit(solution)/shard_map/while/body/eval_jaxpr/dot_general | solution.py:78
  280.8 14.6 %fusion.52 = f32[5,4096]{1,0:T(8,128)S(1)} fusion(f32[5,4096]{1,0:T(8,128)S(1)} %get-tuple-element.298, s32[]{:T(128)S(6)} %select_n.37, f32[5,16384]{1,0:T(8,128)S(1)} %get-tuple-element.308, s32[16384]{0:T(1024)} %bitcast.105, s32[512]{0:T(512)S(1)} %iota_add_fusion.4), kind=kOutput, calls=%fused_computation.7.clone.1 | convolution fusion | flops 511705088 | bytes 608260 | tf_op jit(solution)/shard_map/while/body/eval_jaxpr/dot_general | solution.py:78
  295.4 14.6 %fusion.52 = f32[5,4096]{1,0:T(8,128)S(1)} fusion(f32[5,4096]{1,0:T(8,128)S(1)} %get-tuple-element.298, s32[]{:T(128)S(6)} %select_n.37, f32[5,16384]{1,0:T(8,128)S(1)} %get-tuple-element.308, s32[16384]{0:T(1024)} %bitcast.105, s32[512]{0:T(512)S(1)} %iota_add_fusion.4), kind=kOutput, calls=%fused_computation.7.clone.1 | convolution fusion | flops 511705088 | bytes 608260 | tf_op jit(solution)/shard_map/while/body/eval_jaxpr/dot_general | solution.py:78
  310.0 14.6 %fusion.52 = f32[5,4096]{1,0:T(8,128)S(1)} fusion(f32[5,4096]{1,0:T(8,128)S(1)} %get-tuple-element.298, s32[]{:T(128)S(6)} %select_n.37, f32[5,16384]{1,0:T(8,128)S(1)} %get-tuple-element.308, s32[16384]{0:T(1024)} %bitcast.105, s32[512]{0:T(512)S(1)} %iota_add_fusion.4), kind=kOutput, calls=%fused_computation.7.clone.1 | convolution fusion | flops 511705088 | bytes 608260 | tf_op jit(solution)/shard_map/while/body/eval_jaxpr/dot_general | solution.py:78
  324.7 4.9 %collective-permute-start = (f32[5,1,128]{2,1,0:T(1,128)S(1)}, f32[5,1,128]{2,1,0:T(1,128)S(1)}, u32[]{:S(2)}, u32[]{:S(2)}) collective-permute-start(f32[5,1,128]{2,1,0:T(1,128)S(1)} %get-tuple-element.212), channel_id=1, source_target_pairs={{4,0},{8,4},{12,8},{16,12},{20,16},{24,20},{28,24},{5,1},{9,5},{13... | collective-permute-start | bytes 7688 | tf_op jit(solution)/shard_map/ppermute | solution.py:24
  329.6 1.9 collective-permute-start.1
  331.5 3.3 collective-permute-done.1
  334.9 3.6 %collective-permute-start.2 = (f32[5,34,1]{2,1,0:T(8,128)S(1)}, f32[5,34,1]{2,1,0:T(8,128)S(1)}, u32[]{:S(2)}, u32[]{:S(2)}) collective-permute-start(f32[5,34,1]{2,1,0:T(8,128)S(1)} %get-tuple-element.209), channel_id=1, source_target_pairs={{1,0},{2,1},{3,2},{5,4},{6,5},{7,6},{9,8},{10,9},{11,10},{13,12},{... | collective-permute-start | bytes 2048 | tf_op jit(solution)/shard_map/ppermute | solution.py:24
  338.5 3.3 collective-permute-start.3
  342.2 1.3 collective-permute-done.3
  (81 shorter events, 18.0 us)
Async XLA Ops:
  0.6 198.2 %copy-start = (f32[8,16]{1,0:T(8,128)S(1)}, f32[8,16]{1,0:T(8,128)}, u32[]{:S(2)}) copy-start(f32[8,16]{1,0:T(8,128)} %param.15) | copy-start | bytes 1540
  15.1 25.9 %copy-start.2 = (f32[16,4096]{1,0:T(8,128)S(1)}, f32[16,4096]{1,0:T(8,128)}, u32[]{:S(2)}) copy-start(f32[16,4096]{1,0:T(8,128)} %param.11) | copy-start | bytes 786436
  35.3 42.8 %all-to-all-start = ((s32[2,8,4,512]{3,2,0,1:T(4,128)}), s32[2,8,4,512]{3,2,0,1:T(4,128)}, u32[]{:S(2)}, u32[]{:S(2)}) async-start(s32[2,8,4,512]{3,2,0,1:T(4,128)} %copy.30), calls=%async_computation | async-start | bytes 262144 | tf_op jit(solution)/shard_map/all_to_all | solution.py:120
  79.7 8.1 %all-to-all-start.1 = ((s32[2,8,4,512]{3,1,0,2:T(8,128)}), s32[2,8,4,512]{3,1,0,2:T(8,128)S(1)}, u32[]{:S(2)}, u32[]{:S(2)}) async-start(s32[2,8,4,512]{3,1,0,2:T(8,128)} %copy.31), calls=%async_computation.1 | async-start | bytes 262144 | tf_op jit(solution)/shard_map/all_to_all | solution.py:119
  87.8 28.1 %all-to-all-start.2 = ((f32[8,16,1,4,512]{4,3,1,2,0:T(4,128)}), f32[8,16,1,4,512]{4,3,1,2,0:T(4,128)S(1)}, u32[]{:S(2)}, u32[]{:S(2)}) async-start(f32[8,16,1,4,512]{4,3,1,2,0:T(4,128)} %bitcast_dynamic-update-slice_fusion), calls=%async_computation.2 | async-start | bytes 2097152 | tf_op jit(solution)/shard_map/all_to_all | solution.py:12
  117.5 82.0 %all-to-all-start.3 = ((f32[16,8,4,512]{3,1,0,2:T(8,128)}), f32[16,8,4,512]{3,1,0,2:T(8,128)S(1)}, u32[]{:S(2)}, u32[]{:S(2)}) async-start(f32[16,8,4,512]{3,1,0,2:T(8,128)} %copy.42), calls=%async_computation.3 | async-start | bytes 2097152 | tf_op jit(solution)/shard_map/all_to_all | solution.py:112
  198.0 2.8 copy-start.1
  207.6 136.0 %copy-start.3 = (f32[4,32,128]{2,1,0:T(8,128)S(1)}, f32[4,32,128]{2,1,0:T(8,128)}, u32[]{:S(2)}) copy-start(f32[4,32,128]{2,1,0:T(8,128)} %param.17) | copy-start | bytes 196612
  207.6 136.6 %copy-start.4 = (f32[32,128]{1,0:T(8,128)S(1)}, f32[32,128]{1,0:T(8,128)}, u32[]{:S(2)}) copy-start(f32[32,128]{1,0:T(8,128)} %param.16) | copy-start | bytes 49156
  324.7 6.8 %collective-permute-start = (f32[5,1,128]{2,1,0:T(1,128)S(1)}, f32[5,1,128]{2,1,0:T(1,128)S(1)}, u32[]{:S(2)}, u32[]{:S(2)}) collective-permute-start(f32[5,1,128]{2,1,0:T(1,128)S(1)} %get-tuple-element.212), channel_id=1, source_target_pairs={{4,0},{8,4},{12,8},{16,12},{20,16},{24,20},{28,24},{5,1},{9,5},{13... | collective-permute-start | bytes 7688 | tf_op jit(solution)/shard_map/ppermute | solution.py:24
  329.6 5.2 %collective-permute-start.1 = (f32[5,1,128]{2,1,0:T(1,128)S(1)}, f32[5,1,128]{2,1,0:T(1,128)S(1)}, u32[]{:S(2)}, u32[]{:S(2)}) collective-permute-start(f32[5,1,128]{2,1,0:T(1,128)S(1)} %get-tuple-element.211), channel_id=1, source_target_pairs={{0,4},{4,8},{8,12},{12,16},{16,20},{20,24},{24,28},{1,5},{5,9},{9,... | collective-permute-start | bytes 7688 | tf_op jit(solution)/shard_map/ppermute | solution.py:23
  334.9 7.3 %collective-permute-start.2 = (f32[5,34,1]{2,1,0:T(8,128)S(1)}, f32[5,34,1]{2,1,0:T(8,128)S(1)}, u32[]{:S(2)}, u32[]{:S(2)}) collective-permute-start(f32[5,34,1]{2,1,0:T(8,128)S(1)} %get-tuple-element.209), channel_id=1, source_target_pairs={{1,0},{2,1},{3,2},{5,4},{6,5},{7,6},{9,8},{10,9},{11,10},{13,12},{... | collective-permute-start | bytes 2048 | tf_op jit(solution)/shard_map/ppermute | solution.py:24
  338.5 5.0 %collective-permute-start.3 = (f32[5,34,1]{2,1,0:T(8,128)S(1)}, f32[5,34,1]{2,1,0:T(8,128)S(1)}, u32[]{:S(2)}, u32[]{:S(2)}) collective-permute-start(f32[5,34,1]{2,1,0:T(8,128)S(1)} %get-tuple-element.210), channel_id=1, source_target_pairs={{0,1},{1,2},{2,3},{4,5},{5,6},{6,7},{8,9},{9,10},{10,11},{12,13},{... | collective-permute-start | bytes 2048 | tf_op jit(solution)/shard_map/ppermute | solution.py:23
